TPU v7x, 512 devices: a whole 4x8x8 slice. The times are simulated.
512 devices in a mesh: dp: 128 (over z, x, y_hi, core), mp: 4 (over y_lo).
Axes of the slice: x: 4, y: 8 (y_hi: 2, y_lo: 4; y = y_hi * 4 + y_lo), z: 8, core: 2. Of those that a mesh axis runs over, the one named last changes fastest.
Arguments:
- factor_rows: bfloat16 [4, 128, 128, 768], P('mp', None, 'dp')
- old_statistic: float32 [128, 4, 768, 768], P('dp', 'mp'), may hold values from -1 to 2, as said below
- assignment: int32 [4, 128], P('mp'), may hold values from 0 to 127, each once within a row
- gradient: bfloat16 [128, 4, 768, 512], P('dp', None, None, 'mp'), may hold values from -3 to 3
Outputs:
- update: bfloat16 [128, 4, 768, 512], P('dp', None, None, 'mp')
Inputs may be any that keep to these rules, and one draw needn't show every extreme that they name: Each row of assignment names every block number once. `old_statistic`: each block is symmetric positive definite.
All inputs are finite; a program needn't handle non-finite values.
Results may differ from a plain program's by a relative error of at most 0.001.
The roundings to bfloat16 on the way count: a program that leaves them out, or rounds other values in their place, can miss the bound.
Values may be sent and summed in bfloat16 or wider, within the bound.
A program may use at most 64 MiB of HBM per device.

v0:
```python
import jax
import jax.numpy as jnp
from jax import lax
from jax.sharding import PartitionSpec as P


def cut_along(x, dim, size):
    dims = x.shape
    pieces = x.reshape(*dims[:dim], size, dims[dim] // size, *dims[dim + 1 :])
    return jnp.moveaxis(pieces, dim, 0)


def piece_ends(length, count):
    unit = 8 if length >= 8 * count else 1
    return [length // unit * k // count * unit for k in range(1, count)]


def laid_out(pieces, dim):
    dims = list(pieces.shape[1:])
    dims[dim] *= pieces.shape[0]
    return jnp.moveaxis(pieces, 0, dim).reshape(dims)


def exchange_in_pieces(x, axis, pieces, split_dim, concat_dim):
    blocks = cut_along(x, split_dim, lax.axis_size(axis))
    cut = max(range(1, max(2, blocks.ndim - 1)), key=lambda d: blocks.shape[d])
    finished = []
    for section in jnp.split(blocks, piece_ends(blocks.shape[cut], pieces), axis=cut):
        if section.size:
            finished.append(lax.all_to_all(section, axis, split_axis=0, concat_axis=0, tiled=True))
    return laid_out(jnp.concatenate(finished, axis=cut), concat_dim)


def newton_factors(statistic):
    identity = jnp.eye(statistic.shape[0], dtype=jnp.float32)
    frob_norm = jnp.sqrt(jnp.sum(statistic * statistic) + 1e-06)
    normed = statistic / frob_norm
    step_one = ((5.0 * identity - normed) * 0.25).astype(jnp.bfloat16)
    square_one = jnp.dot(step_one, step_one, preferred_element_type=jnp.float32).astype(
        jnp.bfloat16
    )
    product_one = jnp.dot(
        square_one, normed.astype(jnp.bfloat16), preferred_element_type=jnp.float32
    ).astype(jnp.bfloat16)
    coupled_one = jnp.dot(square_one, product_one, preferred_element_type=jnp.float32)
    step_two = ((5.0 * identity - coupled_one) * 0.25).astype(jnp.bfloat16)
    square_two = jnp.dot(step_two, step_two, preferred_element_type=jnp.float32).astype(
        jnp.bfloat16
    )
    product_two = jnp.dot(
        square_two, coupled_one.astype(jnp.bfloat16), preferred_element_type=jnp.float32
    ).astype(jnp.bfloat16)
    coupled_two = jnp.dot(square_two, product_two, preferred_element_type=jnp.float32)
    step_three = ((5.0 * identity - coupled_two) / (4.0 * jnp.sqrt(jnp.sqrt(frob_norm)))).astype(
        jnp.bfloat16
    )
    return jnp.stack([step_one, step_two, step_three])


def body(factor_rows, old_statistic, assignment, gradient):
    chosen = assignment[0]
    picked = jnp.take(factor_rows[0], chosen, axis=0)
    arrived = lax.all_to_all(picked, "dp", split_axis=0, concat_axis=1, tiled=True)
    factors = arrived[0]
    count = factors.shape[0]
    gram = lax.dot_general(
        factors, factors, (((0,), (0,)), ((), ())), preferred_element_type=jnp.float32
    )
    statistic = old_statistic[0, 0] + gram / count
    stacked = newton_factors(statistic)
    first_pass = jnp.einsum(
        "ij,nkjc->nkic",
        stacked[2],
        lax.all_to_all(gradient, "mp", split_axis=1, concat_axis=3, tiled=True),
        preferred_element_type=jnp.float32,
    ).astype(jnp.bfloat16)
    second_pass = jnp.einsum(
        "ij,nkjc->nkic", stacked[1], first_pass, preferred_element_type=jnp.float32
    ).astype(jnp.bfloat16)
    result = jnp.einsum(
        "ij,nkjc->nkic", stacked[0], second_pass, preferred_element_type=jnp.float32
    ).astype(jnp.bfloat16)
    return exchange_in_pieces(result, "mp", 2, 3, 1)


def solution(mesh):
    return jax.shard_map(
        body,
        mesh=mesh,
        in_specs=(
            P("mp", None, "dp", None),
            P("dp", "mp", None, None),
            P("mp", None),
            P("dp", None, None, "mp"),
        ),
        out_specs=P("dp", None, None, "mp"),
        check_vma=False,
    )
```

profile of v0, /device:TPU:1, one launch (start us, length us, event | category | flops | bytes accessed | tf_op | source)
XLA Modules:
  0.0 100.1 jit_solution(3131647281253693340)
XLA Ops:
  0.0 0.0 copy-start
  0.0 0.7 fusion.17
  0.7 0.7 compare_and_fusion
  1.4 0.0 copy-done
  1.4 0.9 gather_fusion
  2.3 0.1 bitcast_select_fusion
  2.4 0.5 broadcast.86
  2.9 0.7 reduce
  3.6 0.7 reshape.96
  4.4 20.9 %all-to-all-start = ((bf16[128,2,384]{2,1,0:T(2,128)(2,1)}), bf16[128,2,384]{2,1,0:T(2,128)(2,1)S(1)}, u32[]{:S(2)}, u32[]{:S(2)}) async-start(bf16[128,2,384]{2,1,0:T(2,128)(2,1)} %reshape.96), calls=%async_computation | async-start | bytes 393216 | tf_op jit(solution)/shard_map/all_to_all | solution.py:63
  25.2 0.0 copy-done.3
  25.2 1.2 %copy.12 = bf16[1,4,768,128]{2,3,0,1:T(8,128)(2,1)} copy(bf16[1,4,768,128]{3,2,1,0:T(8,128)(2,1)S(1)} %copy-done.3) | data formatting | bytes 1572864 | tf_op args[3]
  26.4 13.8 %all-to-all-done = bf16[128,2,384]{2,1,0:T(2,128)(2,1)S(1)} async-done(((bf16[128,2,384]{2,1,0:T(2,128)(2,1)}), bf16[128,2,384]{2,1,0:T(2,128)(2,1)S(1)}, u32[]{:S(2)}, u32[]{:S(2)}) %all-to-all-start) | async-done | bytes 196640 | tf_op jit(solution)/shard_map/all_to_all | solution.py:63
  40.2 4.2 %all-to-all-start.1 = ((bf16[1,4,768,128]{2,3,0,1:T(8,128)(2,1)}), bf16[1,4,768,128]{2,3,0,1:T(8,128)(2,1)}, u32[]{:S(2)}, u32[]{:S(2)}) async-start(bf16[1,4,768,128]{2,3,0,1:T(8,128)(2,1)} %copy.12), calls=%async_computation.1 | async-start | bytes 1572864 | tf_op jit(solution)/shard_map/all_to_all | solution.py:74
  44.4 0.1 reshape.97
  44.6 3.1 %multiply_reduce_fusion = (f32[]{:T(128)}, f32[768,768]{1,0:T(8,128)S(1)}) fusion(bf16[128,1,768]{2,1,0:T(2,128)(2,1)S(1)} %reshape.97, f32[1,1,768,768]{3,2,1,0:T(8,128)} %param.5), kind=kOutput, calls=%fused_computation.11 | convolution fusion | flops 153354240 | bytes 4915204 | tf_op jit(solution)/shard_map/dot_general | solution.py:66
  48.3 0.3 fusion.1
  48.6 0.0 copy-start.1
  48.6 1.0 %copy-done.1 = bf16[768,768]{1,0:T(8,128)(2,1)} copy-done((bf16[768,768]{1,0:T(8,128)(2,1)}, bf16[768,768]{1,0:T(8,128)(2,1)S(1)}, u32[]{:S(2)}) %copy-start.1) | copy-done | bytes 1179672
  49.6 2.1 %convolution_convert_fusion.3 = bf16[768,768]{1,0:T(8,128)(2,1)} fusion(bf16[768,768]{1,0:T(8,128)(2,1)S(1)} %fusion.1), kind=kOutput, calls=%fused_computation.16 | convolution fusion | flops 906559488 | bytes 2359296 | tf_op jit(solution)/shard_map/dot_general | solution.py:39
  51.8 5.0 %fusion.10 = f32[768,768]{1,0:T(8,128)} fusion(bf16[768,768]{1,0:T(8,128)(2,1)} %convolution_convert_fusion.3, f32[768,768]{1,0:T(8,128)S(1)} %get-tuple-element.8, f32[]{:T(128)S(6)} %sqrt.9), kind=kOutput, calls=%fused_computation.24 | convolution fusion | flops 1813708800 | bytes 5898244 | tf_op jit(solution)/shard_map/dot_general | solution.py:45
  56.9 3.6 %convolution_convert_fusion.1 = bf16[768,768]{1,0:T(8,128)(2,1)S(1)} fusion(f32[768,768]{1,0:T(8,128)} %fusion.10), kind=kOutput, calls=%fused_computation.14 | convolution fusion | flops 909508608 | bytes 3538944 | tf_op jit(solution)/shard_map/dot_general | solution.py:47
  60.5 0.0 copy-done.4
  60.5 2.1 %convolution_convert_fusion = bf16[768,768]{1,0:T(8,128)(2,1)} fusion(bf16[768,768]{1,0:T(8,128)(2,1)S(1)} %convolution_convert_fusion.1, f32[768,768]{1,0:T(8,128)S(1)} %copy-done.4), kind=kOutput, calls=%fused_computation.13 | convolution fusion | flops 907149312 | bytes 4718592 | tf_op jit(solution)/shard_map/dot_general | solution.py:50
  62.7 1.8 %all-to-all-done.1 = bf16[1,4,768,128]{2,3,0,1:T(8,128)(2,1)} async-done(((bf16[1,4,768,128]{2,3,0,1:T(8,128)(2,1)}), bf16[1,4,768,128]{2,3,0,1:T(8,128)(2,1)}, u32[]{:S(2)}, u32[]{:S(2)}) %all-to-all-start.1) | async-done | bytes 786464 | tf_op jit(solution)/shard_map/all_to_all | solution.py:74
  64.5 4.2 %convolution_convert_fusion.6 = bf16[768,512]{1,0:T(8,128)(2,1)} fusion(bf16[768,512]{0,1:T(8,128)(2,1)} %bitcast.8, bf16[768,768]{1,0:T(8,128)(2,1)S(1)} %convolution_convert_fusion.1, bf16[768,768]{1,0:T(8,128)(2,1)} %convolution_convert_fusion, f32[]{:T(128)S(6)} %mul_shard_map.3), kind=kOutput, calls=%fused_computation.19 | convolution fusion | flops 1513291776 | bytes 3932164 | tf_op jit(solution)/shard_map/ij,nkjc->nkic/dot_general | solution.py:71
  68.6 3.4 %convolution_convert_fusion.4 = bf16[512,768]{1,0:T(8,128)(2,1)S(1)} fusion(bf16[768,768]{1,0:T(8,128)(2,1)S(1)} %copy-done.2, bf16[768,512]{1,0:T(8,128)(2,1)} %convolution_convert_fusion.6, f32[768,768]{1,0:T(8,128)} %fusion.10), kind=kOutput, calls=%fused_computation.17 | convolution fusion | flops 1211695104 | bytes 5111808 | tf_op jit(solution)/shard_map/ij,nkjc->nkic/dot_general | solution.py:80
  72.1 0.4 copy.13
  72.5 0.1 fusion.29
  72.5 13.1 %all_to_all.34 = bf16[4,1,1,384,128]{4,3,2,1,0:T(8,128)(2,1)S(1)} all-to-all(bf16[4,1,1,384,128]{4,3,2,1,0:T(8,128)(2,1)S(1)} %get-tuple-element.5), channel_id=1, replica_groups=mesh['dp'=128,'mp'=4] {'mp'}, dimensions={0} | all-to-all | bytes 786432 | tf_op jit(solution)/shard_map/all_to_all | solution.py:30
  85.6 13.6 %all_to_all.35 = bf16[4,1,1,384,128]{4,3,2,1,0:T(8,128)(2,1)S(1)} all-to-all(bf16[4,1,1,384,128]{4,3,2,1,0:T(8,128)(2,1)S(1)} %get-tuple-element.6), channel_id=1, replica_groups=mesh['dp'=128,'mp'=4] {'mp'}, dimensions={0} | all-to-all | bytes 786432 | tf_op jit(solution)/shard_map/all_to_all | solution.py:30
  99.2 0.9 maximum_bitcast_fusion
  (5 shorter events, 0.0 us)
Async XLA Ops:
  0.0 1.4 %copy-start = (bf16[1,128,1,768]{3,1,2,0:T(8,128)(2,1)S(1)}, bf16[1,128,1,768]{3,1,2,0:T(8,128)(2,1)}, u32[]{:S(2)}) copy-start(bf16[1,128,1,768]{3,1,2,0:T(8,128)(2,1)} %param.4) | copy-start | bytes 589828
  0.0 25.2 %copy-start.3 = (bf16[1,4,768,128]{3,2,1,0:T(8,128)(2,1)S(1)}, bf16[1,4,768,128]{3,2,1,0:T(8,128)(2,1)}, u32[]{:S(2)}) copy-start(bf16[1,4,768,128]{3,2,1,0:T(8,128)(2,1)} %param.7) | copy-start | bytes 2359300
  4.4 35.9 %all-to-all-start = ((bf16[128,2,384]{2,1,0:T(2,128)(2,1)}), bf16[128,2,384]{2,1,0:T(2,128)(2,1)S(1)}, u32[]{:S(2)}, u32[]{:S(2)}) async-start(bf16[128,2,384]{2,1,0:T(2,128)(2,1)} %reshape.96), calls=%async_computation | async-start | bytes 393216 | tf_op jit(solution)/shard_map/all_to_all | solution.py:63
  40.2 24.3 %all-to-all-start.1 = ((bf16[1,4,768,128]{2,3,0,1:T(8,128)(2,1)}), bf16[1,4,768,128]{2,3,0,1:T(8,128)(2,1)}, u32[]{:S(2)}, u32[]{:S(2)}) async-start(bf16[1,4,768,128]{2,3,0,1:T(8,128)(2,1)} %copy.12), calls=%async_computation.1 | async-start | bytes 1572864 | tf_op jit(solution)/shard_map/all_to_all | solution.py:74
  48.6 1.0 %copy-start.1 = (bf16[768,768]{1,0:T(8,128)(2,1)}, bf16[768,768]{1,0:T(8,128)(2,1)S(1)}, u32[]{:S(2)}) copy-start(bf16[768,768]{1,0:T(8,128)(2,1)S(1)} %fusion.1) | copy-start | bytes 3538948
  56.9 3.7 %copy-start.4 = (f32[768,768]{1,0:T(8,128)S(1)}, f32[768,768]{1,0:T(8,128)}, u32[]{:S(2)}) copy-start(f32[768,768]{1,0:T(8,128)} %fusion.10) | copy-start | bytes 7077892
  64.5 4.2 %copy-start.2 = (bf16[768,768]{1,0:T(8,128)(2,1)S(1)}, bf16[768,768]{1,0:T(8,128)(2,1)}, u32[]{:S(2)}) copy-start(bf16[768,768]{1,0:T(8,128)(2,1)} %copy-done.1) | copy-start | bytes 3538948
where the time goes:
time: 101 us; the launch traced here: 100 us
  blocking collectives  26.7 us (26%)
  starting transfers between devices  25.1 us (25%)
  matrix products  23.6 us (23%)
  waiting for transfers between devices  15.6 us (15%)
  local copies, waits for them, and re-layouts  4.87 us (5%)
  other arithmetic  3.47 us (3%)
    all_to_all x2, blocking collectives, exchange_in_pieces(): lax.all_to_all(section, axis, split_axis=0, concat_axis=0, tiled=True)  26.7 us
    all_to_all x1, starting transfers between devices, body(): lax.all_to_all(picked, 'dp', split_axis=0, concat_axis=1, tiled=True)  20.9 us
    all_to_all x1, waiting for transfers between devices, body(): lax.all_to_all(picked, 'dp', split_axis=0, concat_axis=1, tiled=True)  13.8 us
    dot_general x1, matrix products, newton_factors(): jnp.dot(square_one, product_one, preferred_element_type=jnp.float32)  5.05 us
    all_to_all x1, starting transfers between devices, body(): lax.all_to_all(gradient, 'mp', split_axis=1, concat_axis=3, tiled=True)  4.2 us
    dot_general x1, matrix products, body(): jnp.einsum('ij,nkjc->nkic', stacked[2], lax.all_to_all(gradient, 'mp', sp...  4.16 us
    dot_general x1, matrix products, newton_factors(): jnp.dot(step_two, step_two, preferred_element_type=jnp.float32)  3.65 us
    dot_general x1, matrix products, body(): jnp.einsum('ij,nkjc->nkic', stacked[0], second_pass, preferred_element_ty...  3.45 us
  transfers between devices with their start and end apart: 2, of which 2 were waited for; matrix products, arithmetic and copies ran while one was open for 18% of the time, Pallas kernels for 0%

commit v1 on v0

v1 whole, which is shorter than its diff:
```python
import jax
import jax.numpy as jnp
from jax import lax
from jax.experimental import pallas as pl
from jax.experimental.pallas import tpu as pltpu
from jax.sharding import PartitionSpec as P

MESH = pl.DeviceIdType.MESH
F32, BF16 = jnp.float32, jnp.bfloat16
TILE = 128
ROWS_PER = 8


def dot(a, b):
    return jnp.dot(a, b, preferred_element_type=F32)


def make_kernel(n_dp, n_mp, order):
    def kernel(
        rows_hbm, old_hbm, assign_hbm, grad_hbm, out_ref,
        rows, assign, stat, wide, sbuf, rbuf, gbuf, rbig,
        normed, step_one, step_two, step_three, square, product, coupled,
        load_sem, send_sem, recv_sem, gsend_sem, grecv_sem, osend_sem, orecv_sem, ready,
    ):
        size = stat.shape[0]
        n_cut = size // TILE
        me, mine = lax.axis_index("dp"), lax.axis_index("mp")

        def peer(d):
            return {"dp": d, "mp": mine}

        def group(m):
            return {"dp": me, "mp": m}

        barrier = pltpu.get_barrier_semaphore()

        def greet(d, carry):
            pl.semaphore_signal(barrier, inc=1, device_id=peer(d), device_id_type=MESH)
            return carry

        others = order(mine)
        for m in others:
            pl.semaphore_signal(barrier, inc=1, device_id=group(m), device_id_type=MESH)
        lax.fori_loop(me + 1, n_dp, greet, 0)

        loads = [
            pltpu.make_async_copy(assign_hbm, assign, load_sem.at[0]),
            pltpu.make_async_copy(rows_hbm, rows, load_sem.at[1]),
            pltpu.make_async_copy(old_hbm, stat, load_sem.at[2]),
            pltpu.make_async_copy(grad_hbm.at[mine], gbuf.at[mine], load_sem.at[3]),
        ]
        for load in loads:
            load.start()

        loads[0].wait()
        loads[1].wait()
        block = lax.broadcasted_iota(jnp.int32, (n_dp, n_dp), 0)
        hot = jnp.where(block == assign[...], 1.0, 0.0).astype(BF16)
        picked = lax.dot_general(
            hot, rows[...], (((0,), (0,)), ((), ())), preferred_element_type=F32
        )
        for j in range(n_cut):
            wide[pl.ds(j, n_dp, stride=ROWS_PER), :] = picked[:, j * TILE : (j + 1) * TILE]
        for j in range(n_cut, ROWS_PER):
            wide[pl.ds(j, n_dp, stride=ROWS_PER), :] = jnp.zeros((n_dp, TILE), F32)
        sbuf[...] = wide[...].astype(BF16).reshape(sbuf.shape)
        rbuf[me] = sbuf[me]

        pl.semaphore_wait(barrier, me + len(others))

        def send(d):
            pltpu.make_async_remote_copy(
                sbuf.at[d], rbuf.at[me], send_sem.at[0], recv_sem.at[0],
                device_id=peer(d), device_id_type=MESH,
            ).start()

        def earlier(d, carry):
            pl.semaphore_signal(ready.at[me], inc=1, device_id=peer(d), device_id_type=MESH)
            send(d)
            return carry

        lax.fori_loop(0, me, earlier, 0)

        arriving = []
        for k, m in enumerate(others):
            copy = pltpu.make_async_remote_copy(
                grad_hbm.at[m], gbuf.at[mine], gsend_sem.at[k], grecv_sem.at[mine],
                device_id=group(m), device_id_type=MESH,
            )
            copy.start()
            arriving.append(copy)

        def later(d, carry):
            pl.semaphore_wait(ready.at[d], 1)
            send(d)
            return carry

        lax.fori_loop(me + 1, n_dp, later, 0)

        all_but_one = rbuf.at[pl.ds(0, n_dp - 1)]
        pltpu.make_async_copy(all_but_one, all_but_one, recv_sem.at[0]).wait()
        wide[...] = rbuf[...].reshape(wide.shape).astype(F32)
        for j in range(n_cut):
            rbig[:, j * TILE : (j + 1) * TILE] = wide[
                pl.ds(j, n_dp, stride=ROWS_PER), :
            ].astype(BF16)

        loads[2].wait()
        step = 256
        cuts = [slice(i, i + step) for i in range(0, size, step)]
        total = jnp.zeros((), F32)
        for cut in cuts:
            gram = lax.dot_general(
                rbig[:, cut], rbig[...], (((0,), (0,)), ((), ())), preferred_element_type=F32
            )
            value = stat[cut, :] + gram * (1.0 / n_dp)
            stat[cut, :] = value
            total = total + jnp.sum(value * value)
        frob = jnp.sqrt(total + 1e-06)
        inverse = 1.0 / frob
        last_scale = 1.0 / (4.0 * jnp.sqrt(jnp.sqrt(frob)))

        def diagonal(cut):
            down = lax.broadcasted_iota(jnp.int32, (step, size), 0) + cut.start
            across = lax.broadcasted_iota(jnp.int32, (step, size), 1)
            return jnp.where(down == across, 5.0, 0.0).astype(F32)

        for cut in cuts:
            value = stat[cut, :] * inverse
            normed[cut, :] = value.astype(BF16)
            step_one[cut, :] = ((diagonal(cut) - value) * 0.25).astype(BF16)
        for cut in cuts:
            square[cut, :] = dot(step_one[cut, :], step_one[...]).astype(BF16)
        for cut in cuts:
            product[cut, :] = dot(square[cut, :], normed[...]).astype(BF16)
        for cut in cuts:
            value = dot(square[cut, :], product[...])
            coupled[cut, :] = value.astype(BF16)
            step_two[cut, :] = ((diagonal(cut) - value) * 0.25).astype(BF16)
        for cut in cuts:
            square[cut, :] = dot(step_two[cut, :], step_two[...]).astype(BF16)
        for cut in cuts:
            product[cut, :] = dot(square[cut, :], coupled[...]).astype(BF16)
        for cut in cuts:
            value = dot(square[cut, :], product[...])
            step_three[cut, :] = ((diagonal(cut) - value) * last_scale).astype(BF16)

        loads[3].wait()

        def arrived(m):
            spot = gbuf.at[m]
            pltpu.make_async_copy(spot, spot, grecv_sem.at[m]).wait()

        def applied(first, second):
            block = jnp.concatenate([gbuf[first], gbuf[second]], axis=1)
            one = dot(step_three[...], block).astype(BF16)
            two = dot(step_two[...], one).astype(BF16)
            three = dot(step_one[...], two).astype(BF16)
            gbuf[first] = three[:, :TILE]
            gbuf[second] = three[:, TILE:]

        leaving = []

        def leave(k, m):
            copy = pltpu.make_async_remote_copy(
                gbuf.at[m], out_ref.at[mine], osend_sem.at[k], orecv_sem.at[mine],
                device_id=group(m), device_id_type=MESH,
            )
            copy.start()
            leaving.append(copy)

        arrived(others[0])
        arrived(others[1])
        applied(others[0], others[1])
        leave(0, others[0])
        leave(1, others[1])
        arrived(others[2])
        applied(others[2], mine)
        leave(2, others[2])
        stay = pltpu.make_async_copy(gbuf.at[mine], out_ref.at[mine], load_sem.at[3])
        stay.start()
        for copy in arriving:
            copy.wait_send()
        sent = sbuf.at[pl.ds(0, n_dp - 1)]
        pltpu.make_async_copy(sent, sent, send_sem.at[0]).wait()
        stay.wait()
        for copy in leaving:
            copy.wait_send()
        for m in others:
            spot = out_ref.at[m]
            pltpu.make_async_copy(spot, spot, orecv_sem.at[m]).wait()

    return kernel


def solution(mesh):
    n_dp, n_mp = mesh.shape["dp"], mesh.shape["mp"]

    def order(m):
        near = 1 + lax.rem(m, 2)
        far = jnp.where(m < 2, 3, 0)
        return near, 6 - m - near - far, far

    def body(factor_rows, old_statistic, assignment, gradient):
        size, cols = gradient.shape[2:]
        any_spec = pl.BlockSpec(memory_space=pl.ANY)
        square = pltpu.VMEM((size, size), BF16)
        result = pl.pallas_call(
            make_kernel(n_dp, n_mp, order),
            out_shape=jax.ShapeDtypeStruct((n_mp, size, cols), BF16),
            in_specs=[any_spec] * 4,
            out_specs=any_spec,
            scratch_shapes=[
                pltpu.VMEM((n_dp, size), BF16),
                pltpu.VMEM((1, n_dp), jnp.int32),
                pltpu.VMEM((size, size), F32),
                pltpu.VMEM((n_dp * ROWS_PER, TILE), F32),
                pltpu.VMEM((n_dp, ROWS_PER, TILE), BF16),
                pltpu.VMEM((n_dp, ROWS_PER, TILE), BF16),
                pltpu.VMEM((n_mp, size, cols), BF16),
                pltpu.VMEM((n_dp, size), BF16),
                square, square, square, square, square, square, square,
                pltpu.SemaphoreType.DMA((4,)),
                pltpu.SemaphoreType.DMA((1,)),
                pltpu.SemaphoreType.DMA((1,)),
                pltpu.SemaphoreType.DMA((n_mp - 1,)),
                pltpu.SemaphoreType.DMA((n_mp,)),
                pltpu.SemaphoreType.DMA((n_mp - 1,)),
                pltpu.SemaphoreType.DMA((n_mp,)),
                pltpu.SemaphoreType.REGULAR((n_dp,)),
            ],
            compiler_params=pltpu.CompilerParams(
                collective_id=0, has_side_effects=True, vmem_limit_bytes=48 * 1024 * 1024
            ),
        )(
            factor_rows.reshape(n_dp, size),
            old_statistic.reshape(size, size),
            assignment,
            gradient.reshape(n_mp, size, cols),
        )
        return result.reshape(gradient.shape)

    return jax.shard_map(
        body,
        mesh=mesh,
        in_specs=(
            P("mp", None, "dp", None),
            P("dp", "mp", None, None),
            P("mp", None),
            P("dp", None, None, "mp"),
        ),
        out_specs=P("dp", None, None, "mp"),
        check_vma=False,
    )
```

time: 101 us -> 62.1 us (0.61)
  the two profiles are of different devices: /device:TPU:1 before, /device:TPU:448 now
where the time goes in v1:
time: 62.1 us; the launch traced here: 61.9 us
  Pallas kernels  56.6 us (91%)
  local copies, waits for them, and re-layouts  5.26 us (8%)
    pallas_call x1, Pallas kernels, body(): pl.pallas_call(make_kernel(n_dp, n_mp, order), out_shape=jax.ShapeDtypeSt...  56.6 us
    unnamed x9, local copies, waits for them, and re-layouts  5.26 us

profile of v1, /device:TPU:448, one launch (start us, length us, event | category | flops | bytes accessed | tf_op | source)
XLA Modules:
  0.0 61.9 jit_solution(15337527388520701565)
XLA Ops:
  0.0 0.0 copy-start
  0.0 1.7 %copy-done = f32[1,1,768,768]{3,2,1,0:T(8,128)S(1)} copy-done((f32[1,1,768,768]{3,2,1,0:T(8,128)S(1)}, f32[1,1,768,768]{3,2,1,0:T(8,128)}, u32[]{:S(2)}) %copy-start) | copy-done | bytes 2359320
  1.7 0.0 copy-start.1
  1.7 1.1 %copy-done.1 = bf16[1,4,768,128]{3,2,1,0:T(8,128)(2,1)S(1)} copy-done((bf16[1,4,768,128]{3,2,1,0:T(8,128)(2,1)S(1)}, bf16[1,4,768,128]{3,2,1,0:T(8,128)(2,1)}, u32[]{:S(2)}) %copy-start.1) | copy-done | bytes 786456
  2.8 0.0 copy-start.2
  2.8 0.9 %copy-done.2 = bf16[1,128,1,768]{3,1,2,0:T(8,128)(2,1)S(1)} copy-done((bf16[1,128,1,768]{3,1,2,0:T(8,128)(2,1)S(1)}, bf16[1,128,1,768]{3,1,2,0:T(8,128)(2,1)}, u32[]{:S(2)}) %copy-start.2) | copy-done | bytes 196632
  3.7 0.0 copy-start.3
  3.7 0.7 %copy-done.3 = s32[1,128]{1,0:T(1,128)S(1)} copy-done((s32[1,128]{1,0:T(1,128)S(1)}, s32[1,128]{1,0:T(1,128)}, u32[]{:S(2)}) %copy-start.3) | copy-done | bytes 536
  4.4 56.6 %shard_map.46 = bf16[4,768,128]{2,1,0:T(8,128)(2,1)S(1)} custom-call(bf16[128,768]{1,0:T(8,128)(2,1)S(1)} %bitcast.7, f32[768,768]{1,0:T(8,128)S(1)} %bitcast.5, s32[1,128]{1,0:T(1,128)S(1)} %copy-done.3, bf16[4,768,128]{2,1,0:T(8,128)(2,1)S(1)} %bitcast.6), custom_call_target="tpu_custom_call" | custom-call | tf_op jit(solution)/shard_map/pallas_call | solution.py:208
  61.0 0.9 %copy.6 = bf16[1,4,768,128]{3,2,1,0:T(8,128)(2,1)} copy(bf16[1,4,768,128]{3,2,1,0:T(8,128)(2,1)S(1)} %bitcast.4) | data formatting | bytes 1572864
Async XLA Ops:
  0.0 1.7 %copy-start = (f32[1,1,768,768]{3,2,1,0:T(8,128)S(1)}, f32[1,1,768,768]{3,2,1,0:T(8,128)}, u32[]{:S(2)}) copy-start(f32[1,1,768,768]{3,2,1,0:T(8,128)} %param.5) | copy-start | bytes 7077892
  1.7 1.1 %copy-start.1 = (bf16[1,4,768,128]{3,2,1,0:T(8,128)(2,1)S(1)}, bf16[1,4,768,128]{3,2,1,0:T(8,128)(2,1)}, u32[]{:S(2)}) copy-start(bf16[1,4,768,128]{3,2,1,0:T(8,128)(2,1)} %param.7) | copy-start | bytes 2359300
  2.8 0.9 %copy-start.2 = (bf16[1,128,1,768]{3,1,2,0:T(8,128)(2,1)S(1)}, bf16[1,128,1,768]{3,1,2,0:T(8,128)(2,1)}, u32[]{:S(2)}) copy-start(bf16[1,128,1,768]{3,1,2,0:T(8,128)(2,1)} %param.4) | copy-start | bytes 589828
  3.7 0.7 %copy-start.3 = (s32[1,128]{1,0:T(1,128)S(1)}, s32[1,128]{1,0:T(1,128)}, u32[]{:S(2)}) copy-start(s32[1,128]{1,0:T(1,128)} %assign_hbm.1) | copy-start | bytes 1540

commit v2 on v1

--- a/solution.py
+++ b/solution.py
@@ -38,11 +38,6 @@
             pl.semaphore_signal(barrier, inc=1, device_id=peer(d), device_id_type=MESH)
             return carry
 
-        others = order(mine)
-        for m in others:
-            pl.semaphore_signal(barrier, inc=1, device_id=group(m), device_id_type=MESH)
-        lax.fori_loop(me + 1, n_dp, greet, 0)
-
         loads = [
             pltpu.make_async_copy(assign_hbm, assign, load_sem.at[0]),
             pltpu.make_async_copy(rows_hbm, rows, load_sem.at[1]),
@@ -51,6 +46,11 @@
         ]
         for load in loads:
             load.start()
+
+        others = order(mine)
+        for m in others:
+            pl.semaphore_signal(barrier, inc=1, device_id=group(m), device_id_type=MESH)
+        lax.fori_loop(me + 1, n_dp, greet, 0)
 
         loads[0].wait()
         loads[1].wait()
@@ -70,7 +70,7 @@
 
         def send(d):
             pltpu.make_async_remote_copy(
-                sbuf.at[d], rbuf.at[me], send_sem.at[0], recv_sem.at[0],
+                sbuf.at[d, pl.ds(0, n_cut)], rbuf.at[me, pl.ds(0, n_cut)], send_sem.at[0], recv_sem.at[0],
                 device_id=peer(d), device_id_type=MESH,
             ).start()
 
@@ -97,7 +97,7 @@
 
         lax.fori_loop(me + 1, n_dp, later, 0)
 
-        all_but_one = rbuf.at[pl.ds(0, n_dp - 1)]
+        all_but_one = rbuf.at[pl.ds(0, n_dp - 1), pl.ds(0, n_cut)]
         pltpu.make_async_copy(all_but_one, all_but_one, recv_sem.at[0]).wait()
         wide[...] = rbuf[...].reshape(wide.shape).astype(F32)
         for j in range(n_cut):
@@ -181,7 +181,7 @@
         stay.start()
         for copy in arriving:
             copy.wait_send()
-        sent = sbuf.at[pl.ds(0, n_dp - 1)]
+        sent = sbuf.at[pl.ds(0, n_dp - 1), pl.ds(0, n_cut)]
         pltpu.make_async_copy(sent, sent, send_sem.at[0]).wait()
         stay.wait()
         for copy in leaving:
@@ -230,7 +230,7 @@
                 pltpu.SemaphoreType.REGULAR((n_dp,)),
             ],
             compiler_params=pltpu.CompilerParams(
-                collective_id=0, has_side_effects=True, vmem_limit_bytes=48 * 1024 * 1024
+                collective_id=0, has_side_effects=True, vmem_limit_bytes=66000000
             ),
         )(
             factor_rows.reshape(n_dp, size),

time: 62.1 us -> 59 us (0.950)
  the two profiles are of different devices: /device:TPU:448 before, /device:TPU:472 now
where the time goes in v2:
time: 59 us; the launch traced here: 58.8 us
  Pallas kernels  56.8 us (96%)
  local copies, waits for them, and re-layouts  2.06 us (3%)
    pallas_call x1, Pallas kernels, body(): pl.pallas_call(make_kernel(n_dp, n_mp, order), out_shape=jax.ShapeDtypeSt...  56.8 us
    unnamed x1, local copies, waits for them, and re-layouts  2.06 us

profile of v2, /device:TPU:472, one launch (start us, length us, event | category | flops | bytes accessed | tf_op | source)
XLA Modules:
  0.0 58.8 jit_solution(16763475427204800471)
XLA Ops:
  0.0 56.8 %shard_map.46 = bf16[4,768,128]{2,1,0:T(8,128)(2,1)} custom-call(bf16[128,768]{1,0:T(8,128)(2,1)} %bitcast.7, f32[768,768]{1,0:T(8,128)} %bitcast.5, s32[1,128]{1,0:T(1,128)} %assign_hbm.1, bf16[4,768,128]{2,1,0:T(8,128)(2,1)} %bitcast.6), custom_call_target="tpu_custom_call" | custom-call | tf_op jit(solution)/shard_map/pallas_call | solution.py:208
  56.8 2.1 %copy.6 = bf16[1,4,768,128]{3,2,1,0:T(8,128)(2,1)} copy(bf16[1,4,768,128]{3,2,1,0:T(8,128)(2,1)} %bitcast.4) | data formatting | bytes 1572864

commit v3 on v2

--- a/solution.py
+++ b/solution.py
@@ -82,13 +82,17 @@
         lax.fori_loop(0, me, earlier, 0)
 
         arriving = []
-        for k, m in enumerate(others):
+
+        def share(k):
             copy = pltpu.make_async_remote_copy(
-                grad_hbm.at[m], gbuf.at[mine], gsend_sem.at[k], grecv_sem.at[mine],
-                device_id=group(m), device_id_type=MESH,
+                grad_hbm.at[others[k]], gbuf.at[mine], gsend_sem.at[k], grecv_sem.at[mine],
+                device_id=group(others[k]), device_id_type=MESH,
             )
             copy.start()
             arriving.append(copy)
+
+        share(0)
+        share(1)
 
         def later(d, carry):
             pl.semaphore_wait(ready.at[d], 1)
@@ -96,6 +100,7 @@
             return carry
 
         lax.fori_loop(me + 1, n_dp, later, 0)
+        share(2)
 
         all_but_one = rbuf.at[pl.ds(0, n_dp - 1), pl.ds(0, n_cut)]
         pltpu.make_async_copy(all_but_one, all_but_one, recv_sem.at[0]).wait()

time: 59 us -> 56 us (0.949)
  the two profiles are of different devices: /device:TPU:472 before, /device:TPU:448 now
where the time goes in v3:
time: 56 us; the launch traced here: 55.8 us
  Pallas kernels  53.7 us (96%)
  local copies, waits for them, and re-layouts  2.06 us (4%)
    pallas_call x1, Pallas kernels, body(): pl.pallas_call(make_kernel(n_dp, n_mp, order), out_shape=jax.ShapeDtypeSt...  53.7 us
    unnamed x1, local copies, waits for them, and re-layouts  2.06 us

profile of v3, /device:TPU:448, one launch (start us, length us, event | category | flops | bytes accessed | tf_op | source)
XLA Modules:
  0.0 55.8 jit_solution(12028048326910508133)
XLA Ops:
  0.0 53.7 %shard_map.46 = bf16[4,768,128]{2,1,0:T(8,128)(2,1)} custom-call(bf16[128,768]{1,0:T(8,128)(2,1)} %bitcast.7, f32[768,768]{1,0:T(8,128)} %bitcast.5, s32[1,128]{1,0:T(1,128)} %assign_hbm.1, bf16[4,768,128]{2,1,0:T(8,128)(2,1)} %bitcast.6), custom_call_target="tpu_custom_call" | custom-call | tf_op jit(solution)/shard_map/pallas_call | solution.py:213
  53.8 2.1 %copy.6 = bf16[1,4,768,128]{3,2,1,0:T(8,128)(2,1)} copy(bf16[1,4,768,128]{3,2,1,0:T(8,128)(2,1)} %bitcast.4) | data formatting | bytes 1572864
